TPU v7x, 32 devices: a whole 2x2x4 slice. The times are simulated.
32 devices in a mesh: dp: 1, sp: 32 (over x, y, z, core).
Axes of the slice: x: 2, y: 2, z: 4, core: 2. Of those that a mesh axis runs over, the one named last changes fastest.
Arguments:
- q: bfloat16 [32, 16, 128], P('dp')
- k: bfloat16 [32, 8192, 16, 128], P('dp', 'sp')
- v: bfloat16 [32, 8192, 16, 128], P('dp', 'sp')
Outputs:
- q: bfloat16 [32, 16, 128], P('dp')
All inputs are finite; a program needn't handle non-finite values.
Results may differ from a plain program's by a relative error of at most 0.012.
Values are sent between devices in bfloat16 or wider.
A program may use at most 2 GiB of HBM per device.

v0:
```python
import jax
import jax.numpy as jnp
from jax import lax
from jax.sharding import PartitionSpec as P


def einsum(form, a, b):
    return jnp.einsum(form, a.astype(jnp.float32), b.astype(jnp.float32))


def part_of(q, k, v):
    grouped = q.reshape(q.shape[0], k.shape[2], -1, q.shape[2])
    scores = einsum("bgsd,bugd->bgsu", grouped, k) * q.shape[2] ** -0.5
    high = jnp.max(scores, -1, keepdims=True)
    weights = jnp.exp(scores - high)
    seen = einsum("bgsu,bugd->bgsd", weights.astype(jnp.bfloat16), v)
    return jnp.concatenate([seen, jnp.sum(weights, -1, keepdims=True), high], -1)


def together(parts):
    seen, total, high = parts[..., :-2], parts[..., -2:-1], parts[..., -1:]
    scale = jnp.exp(high - jnp.max(high, 0))
    return (jnp.sum(seen * scale, 0) / jnp.sum(total * scale, 0)).astype(jnp.bfloat16)


def solution(mesh):
    def step(q, k, v):
        return together(lax.all_gather(part_of(q, k, v), "sp")).reshape(q.shape)

    return jax.shard_map(
        step,
        mesh=mesh,
        in_specs=(P("dp", None, None), P("dp", "sp", None, None), P("dp", "sp", None, None)),
        out_specs=P("dp", None, None),
        check_vma=False,
    )
```

profile of v0, /device:TPU:0, one launch (start us, length us, event | category | flops | bytes accessed | tf_op | source)
XLA Modules:
  0.0 199.4 jit_solution(13150449018337048961)
XLA Ops:
  6.5 0.0 all-gather.3.cloned.1.call-start
  6.5 18.1 %fusion.2 = f32[32,16,1,256]{3,2,1,0:T(1,128)S(1)} fusion(bf16[32,256,16,128]{3,2,1,0:T(8,128)(2,1)} %param.4, bf16[32,16,128,1]{2,1,0,3:T(8,128)(2,1)} %bitcast.25), kind=kOutput, calls=%fused_computation.2 | convolution fusion | flops 33554432 | bytes 34209792 | tf_op jit(solution)/shard_map/bgsd,bugd->bgsu/dot_general | solution.py:8
  24.6 0.1 fusion.9
  24.8 0.3 fusion.10
  25.1 0.3 copy.23
  25.3 0.3 copy.22
  25.6 19.2 %fusion = f32[32,16,1,128]{3,2,1,0:T(1,128)S(1)} fusion(bf16[32,256,16,128]{3,2,1,0:T(8,128)(2,1)} %param.5, bf16[32,16,256,1]{2,1,0,3:T(8,128)(2,1)S(1)} %get-tuple-element.7), kind=kOutput, calls=%fused_computation | convolution fusion | flops 33554432 | bytes 34078720 | tf_op jit(solution)/shard_map/bgsu,bugd->bgsd/dot_general | solution.py:8
  44.8 0.9 pad_maximum_fusion
  45.7 0.0 all-gather.3.cloned.1.call-update
  45.7 117.1 %all-gather.3.cloned.1.call-done = f32[1024,16,1,130]{3,1,2,0:T(8,128)} async-done(((f32[32,16,1,130]{3,1,2,0:T(8,128)}), f32[1024,16,1,130]{3,1,2,0:T(8,128)}) %all-gather.3.cloned.1.call-update) | async-done | bytes 8519696 | tf_op jit(solution)/shard_map/all_gather | solution.py:28
  162.8 5.7 %slice_reduce_fusion = f32[32,16]{1,0:T(8,128)S(1)} fusion(f32[32,32,16,1,130]{4,2,1,0,3:T(8,128)} %bitcast.21), kind=kLoop, calls=%fused_computation.9 | loop fusion | flops 15872 | bytes 67584 | tf_op jit(solution)/shard_map/reduce_max | solution.py:22
  168.5 9.5 %fusion.4 = (f32[32,16]{1,0:T(8,128)S(1)}, f32[32,32,16,1,1]{4,2,1,0,3:T(8,128)}) fusion(f32[32,32,16,1,130]{4,2,1,0,3:T(8,128)} %bitcast.22, f32[32,16]{1,0:T(8,128)S(1)} %slice_reduce_fusion), kind=kLoop, calls=%fused_computation.5 | loop fusion | flops 48640 | bytes 200704 | tf_op jit(solution)/shard_map/reduce_sum | solution.py:23
  178.0 8.4 %copy.36 = f32[32,32,16,1,1]{2,1,0,3,4:T(8,128)S(1)} copy(f32[32,32,16,1,1]{4,2,1,0,3:T(8,128)} %get-tuple-element.6) | data formatting | bytes 131072 | tf_op jit(solution)/shard_map/mul | solution.py:23
  186.5 5.3 %fusion.5 = f32[32,16,128]{2,1,0:T(8,128)S(1)} fusion(f32[32,32,16,1,130]{4,2,1,0,3:T(8,128)} %bitcast.23, f32[32,32,16]{2,1,0:T(8,128)S(1)} %bitcast.24), kind=kLoop, calls=%fused_computation.7 | loop fusion | flops 4128768 | bytes 8716288 | tf_op jit(solution)/shard_map/reduce_sum | solution.py:23
  191.8 0.8 divide_convert_fusion
Async XLA Ops:
  6.5 156.3 %all-gather.3.cloned.1.call-start = ((), (), s32[]{:S(2)}) async-start(), calls=%async_computation | async-start | bytes 17301504 | tf_op jit(solution)/shard_map/all_gather | solution.py:28
Sparse Core Ops, SparseCore 0:
  45.9 116.9 all-gather.2
where the time goes:
time: 200 us; the launch traced here: 199 us
  waiting for transfers between devices  117 us (58%)
  matrix products  37.3 us (19%)
  other arithmetic  22.6 us (11%)
  between operations  13.4 us (7%)
  local copies, waits for them, and re-layouts  8.95 us (4%)
    all_gather x1, waiting for transfers between devices, step(): return together(lax.all_gather(part_of(q, k, v), 'sp')).reshape(q.shape)  117 us
    dot_general x2, matrix products, einsum(): return jnp.einsum(form, a.astype(jnp.float32), b.astype(jnp.float32))  37.3 us
    reduce_sum x1, other arithmetic, together(): jnp.sum(total * scale, 0)  9.47 us
    mul x1, local copies, waits for them, and re-layouts, together(): seen * scale  8.43 us
    reduce_max x1, other arithmetic, together(): scale = jnp.exp(high - jnp.max(high, 0))  5.69 us
    reduce_sum x1, other arithmetic, together(): jnp.sum(seen * scale, 0) / jnp.sum(total * scale, 0)  5.32 us
  transfers between devices with their start and end apart: 1, of which 1 were waited for; matrix products, arithmetic and copies ran while one was open for 0% of the time, Pallas kernels for 0%

commit v1 on v0

v1 whole, which is shorter than its diff:
```python
import functools

import jax
import jax.numpy as jnp
from jax import lax
from jax.experimental import pallas as pl
from jax.experimental.pallas import tpu as pltpu
from jax.sharding import PartitionSpec as P

MESH = pl.DeviceIdType.MESH
SLOTS = 8
LANES = 128


def kernel(n, scale, q_ref, k_hbm, v_hbm, out_ref, kbuf, vbuf, s0, s1, seen_out, stat_out, seen_in, stat_in, ksem, vsem, seen_ssem, stat_ssem, seen_rsem, stat_rsem, out_ssem, out_rsem):
    me = lax.axis_index("sp")
    batch, tokens, heads, head = k_hbm.shape
    half = tokens * heads // 2
    slots = kbuf.shape[0]
    bits = (n - 1).bit_length()

    def peer(x):
        there = me
        for bit in range(bits):
            mine, flip = (me // 2**bit) % 2, (x // 2**bit) % 2
            there = there + flip * (1 - 2 * mine) * 2**bit
        return there

    def owner(i):
        return peer(n - 1 - i)

    def copy_k(i):
        slot = lax.rem(i, slots)
        return pltpu.make_async_copy(k_hbm.at[owner(i)], kbuf.at[slot], ksem.at[slot])

    def copy_v(i):
        slot = lax.rem(i, slots)
        return pltpu.make_async_copy(v_hbm.at[owner(i)], vbuf.at[slot], vsem.at[slot])

    def send_seen(x, there):
        return pltpu.make_async_remote_copy(seen_out.at[x], seen_in.at[x], seen_ssem.at[x], seen_rsem.at[x], device_id={"sp": there}, device_id_type=MESH)

    def send_stat(x, there):
        return pltpu.make_async_remote_copy(stat_out.at[x], stat_in.at[x], stat_ssem.at[x], stat_rsem.at[x], device_id={"sp": there}, device_id_type=MESH)

    def send_out(x, there):
        return pltpu.make_async_remote_copy(out_ref.at[me], out_ref.at[me], out_ssem.at[x], out_rsem.at[x], device_id={"sp": there}, device_id_type=MESH)

    copy_k(0).start()
    for i in range(slots - 1):
        copy_k(i + 1).start()
        copy_v(i).start()
    copy_v(slots - 1).start()

    barrier = pltpu.get_barrier_semaphore()

    @pl.loop(1, n)
    def _(x):
        pl.semaphore_signal(barrier, inc=1, device_id={"sp": peer(x)}, device_id_type=MESH)

    rows = lax.broadcasted_iota(jnp.int32, (2 * heads, LANES), 0)
    lanes = lax.broadcasted_iota(jnp.int32, (2 * heads, LANES), 1)
    bias = jnp.where(rows % heads == lanes % heads, 0.0, -jnp.inf).astype(jnp.float32)
    factor = scale * 1.4426950408889634

    def scores(i, s_ref):
        q = q_ref[owner(i)]
        zero = jnp.zeros_like(q)
        q2 = jnp.concatenate([jnp.concatenate([q, zero], 1), jnp.concatenate([zero, q], 1)], 0)
        k = kbuf[lax.rem(i, slots)].reshape(2, half, head)
        k2 = jnp.concatenate([k[0], k[1]], 1)
        s_ref[...] = lax.dot_general(q2, k2, (((1,), (1,)), ((), ())), preferred_element_type=jnp.float32)

    def weigh(s_ref):
        tiles = [s_ref[:, t : t + LANES] + bias for t in range(0, half, LANES)]
        high = functools.reduce(jnp.maximum, tiles)
        high = jnp.max(jnp.maximum(high[:heads], high[heads:]), 1, keepdims=True)
        both = jnp.concatenate([high, high], 0)
        weights = [jnp.exp2((t - both) * factor) for t in tiles]
        total = functools.reduce(jnp.add, weights)
        total = jnp.sum(total[:heads] + total[heads:], 1, keepdims=True)
        return jnp.concatenate([w.astype(jnp.bfloat16) for w in weights], 1), high, total

    def values(i, weights):
        v = vbuf[lax.rem(i, slots)].reshape(2, half, head)
        v2 = jnp.concatenate([v[0], v[1]], 1)
        seen = jnp.dot(weights, v2, preferred_element_type=jnp.float32)
        return seen[:heads, :head] + seen[heads:, head:]

    lane = lax.broadcasted_iota(jnp.int32, (heads // 2, LANES), 1)

    def part(i, s_ref):
        weights, high, total = weigh(s_ref)
        seen = values(i, weights)
        x = n - 1 - i
        h = heads // 2
        seen_out[x] = seen.astype(jnp.bfloat16)
        stat_out[x] = jnp.where(lane < 32, high[:h], jnp.where(lane < 64, high[h:], jnp.where(lane < 96, total[:h], total[h:])))
        there = peer(x)
        send_seen(x, there).start()
        send_stat(x, there).start()

    def step(i, s_now, s_next):
        copy_k(i + 1).wait()
        scores(i + 1, s_next)
        copy_v(i).wait()
        part(i, s_now)

    def refill(i):
        @pl.when(i + slots < n)
        def _():
            copy_k(i + slots).start()

        @pl.when((i >= 1) & (i - 1 + slots < n))
        def _():
            copy_v(i - 1 + slots).start()

    copy_k(0).wait()
    scores(0, s0)
    pl.semaphore_wait(barrier, n - 1)

    @pl.loop(0, n // 2 - 1)
    def _(j):
        i = 2 * j
        refill(i)
        step(i, s0, s1)
        refill(i + 1)
        step(i + 1, s1, s0)

    i = n - 2
    step(i, s0, s1)

    weights, high, total = weigh(s1)
    copy_v(n - 1).wait()
    seen = values(n - 1, weights)

    @pl.loop(1, n)
    def _(x):
        there = peer(x)
        send_stat(x, there).wait_recv()
        send_seen(x, there).wait_recv()

    top = functools.reduce(jnp.maximum, [stat_in[x] for x in range(1, n)])
    sums = jnp.zeros((heads // 2, LANES), jnp.float32)
    acc = jnp.zeros((heads, head), jnp.float32)
    for x in range(1, n):
        stat = stat_in[x]
        w = jnp.exp2((stat - top) * factor)
        sums += pltpu.roll(w, LANES // 2, 1) * stat
        acc += seen_in[x].astype(jnp.float32) * jnp.concatenate([w[:, 0:1], w[:, 32:33]], 0)
    top = jnp.concatenate([top[:, 0:1], top[:, 32:33]], 0)
    sums = jnp.concatenate([sums[:, 64:65], sums[:, 96:97]], 0)
    new = jnp.maximum(top, high)
    theirs, mine = jnp.exp2((top - new) * factor), jnp.exp2((high - new) * factor)
    result = (acc * theirs + seen * mine) / (sums * theirs + total * mine)
    out_ref[me] = result.astype(jnp.bfloat16)

    @pl.loop(0, n - 1)
    def _(i):
        send_out(n - 1 - i, owner(i)).start()

    @pl.loop(1, n)
    def _(x):
        there = peer(x)
        copy = send_out(x, there)
        copy.wait_send()
        send_seen(x, there).wait_send()
        send_stat(x, there).wait_send()
        pltpu.make_async_remote_copy(out_ref.at[there], out_ref.at[there], out_ssem.at[x], out_rsem.at[x], device_id={"sp": there}, device_id_type=MESH).wait_recv()


def solution(mesh):
    n = mesh.shape["sp"]

    def step(q, k, v):
        batch, tokens, heads, head = k.shape
        rows = tokens * heads // 2
        return pl.pallas_call(
            functools.partial(kernel, n, head**-0.5),
            out_shape=jax.ShapeDtypeStruct(q.shape, q.dtype),
            in_specs=[pl.BlockSpec(memory_space=pltpu.VMEM), pl.BlockSpec(memory_space=pl.ANY), pl.BlockSpec(memory_space=pl.ANY)],
            out_specs=pl.BlockSpec(memory_space=pltpu.VMEM),
            scratch_shapes=[
                pltpu.VMEM((SLOTS, tokens, heads, head), k.dtype),
                pltpu.VMEM((SLOTS, tokens, heads, head), v.dtype),
                pltpu.VMEM((2 * heads, rows), jnp.float32),
                pltpu.VMEM((2 * heads, rows), jnp.float32),
                pltpu.VMEM((n, heads, head), jnp.bfloat16),
                pltpu.VMEM((n, heads // 2, LANES), jnp.float32),
                pltpu.VMEM((n, heads, head), jnp.bfloat16),
                pltpu.VMEM((n, heads // 2, LANES), jnp.float32),
                pltpu.SemaphoreType.DMA((SLOTS,)),
                pltpu.SemaphoreType.DMA((SLOTS,)),
                pltpu.SemaphoreType.DMA((n,)),
                pltpu.SemaphoreType.DMA((n,)),
                pltpu.SemaphoreType.DMA((n,)),
                pltpu.SemaphoreType.DMA((n,)),
                pltpu.SemaphoreType.DMA((n,)),
                pltpu.SemaphoreType.DMA((n,)),
            ],
            compiler_params=pltpu.CompilerParams(collective_id=0, has_side_effects=True, vmem_limit_bytes=60 * 2**20),
        )(q, k, v)

    return jax.shard_map(
        step,
        mesh=mesh,
        in_specs=(P("dp", None, None), P("dp", "sp", None, None), P("dp", "sp", None, None)),
        out_specs=P("dp", None, None),
        check_vma=False,
    )
```

time: 200 us -> 52.6 us (0.26)
  waiting for transfers between devices: 117 us -> 0 us
  Pallas kernels: 0 us -> 50.9 us
  matrix products: 37.3 us -> 0 us
  other arithmetic: 22.6 us -> 0 us
  between operations: 13.4 us -> 0.01 us
  local copies, waits for them, and re-layouts: 8.95 us -> 1.57 us
    all_gather x1 -> x0, waiting for transfers between devices: 117 us -> none  [step(): return together(lax.all_gather(part_of(q, k, v), 'sp')).reshape(q.shape)]
    pallas_call x0 -> x1, Pallas kernels: none -> 50.9 us  [step(): pl.pallas_call(functools.partial(kernel, n, head ** (-0.5)), out_shape=ja...]
    dot_general x2 -> x0, matrix products: 37.3 us -> none  [einsum(): return jnp.einsum(form, a.astype(jnp.float32), b.astype(jnp.float32))]
    reduce_sum x2 -> x0, other arithmetic: 14.8 us -> none  [the longest x1 9.47 us: together(): jnp.sum(total * scale, 0)]
    mul x1 -> x0, local copies, waits for them, and re-layouts: 8.43 us -> none  [together(): seen * scale]
    reduce_max x2 -> x0, other arithmetic: 5.84 us -> none  [the longest x1 5.69 us: together(): scale = jnp.exp(high - jnp.max(high, 0))]
  transfers between devices with their start and end apart: 1 -> 0, of which waited for: 1 -> 0; matrix products, arithmetic and copies ran while one was open for 0% -> 0% of each run, Pallas kernels for 0% -> 0%
where the time goes in v1:
time: 52.6 us; the launch traced here: 52.5 us
  Pallas kernels  50.9 us (97%)
  local copies, waits for them, and re-layouts  1.57 us (3%)
    pallas_call x1, Pallas kernels, step(): pl.pallas_call(functools.partial(kernel, n, head ** (-0.5)), out_shape=ja...  50.9 us
    unnamed x1, local copies, waits for them, and re-layouts  1.57 us

profile of v1, /device:TPU:0, one launch (start us, length us, event | category | flops | bytes accessed | tf_op | source)
XLA Modules:
  0.0 52.5 jit_solution(4516779387017747725)
XLA Ops:
  0.0 50.9 %shard_map.37 = bf16[32,16,128]{2,1,0:T(8,128)(2,1)} custom-call(bf16[32,16,128]{2,1,0:T(8,128)(2,1)} %q_ref.1, bf16[32,256,16,128]{3,2,1,0:T(8,128)(2,1)} %k_hbm.1, bf16[32,256,16,128]{3,2,1,0:T(8,128)(2,1)} %v_hbm.1), custom_call_target="tpu_custom_call" | custom-call | tf_op jit(solution)/shard_map/pallas_call | solution.py:178
  50.9 1.6 %copy.5 = bf16[32,16,128]{2,1,0:T(8,128)(2,1)} copy(bf16[32,16,128]{2,1,0:T(8,128)(2,1)} %shard_map.37) | data formatting | bytes 262144

commit v2 on v0

v2 whole, which is shorter than its diff:
```python
import functools

import jax
import jax.numpy as jnp
from jax import lax
from jax.experimental import pallas as pl
from jax.experimental.pallas import tpu as pltpu
from jax.sharding import PartitionSpec as P

MESH = pl.DeviceIdType.MESH
SLOTS = 4
UNROLL = 4
GREET = 8
PIECES = 4
LANES = 128


def kernel(n, scale, q_hbm, k_hbm, v_hbm, out_ref, q_ref, kbuf, vbuf, s0, s1, seen_out, stat_out, seen_in, stat_in, acc_ref, top_ref, sums_ref, mine, qsem, ksem, vsem, psem, part_ssem, seen_rsem, stat_rsem, out_ssem, out_rsem):
    me = lax.axis_index("sp")
    batch, _, tokens, heads, head = k_hbm.shape
    half = tokens * heads
    bits = (n - 1).bit_length()
    low = UNROLL.bit_length() - 1
    turn = [(1 - 2 * ((me // 2**b) % 2)) * 2**b for b in range(bits)]
    groups = [range(2**b, 2 ** (b + 1)) for b in range(1, bits)]
    groups[0] = range(1, 4)

    def group_of(x):
        return max(x.bit_length() - 2, 0)

    def peer(x):
        return sum((turn[b] for b in range(bits) if x >> b & 1), me)

    def block(j):
        if isinstance(j, int):
            return peer((n - 1 - UNROLL * j) >> low << low)
        there, rest = me, n // UNROLL - 1 - j
        for b in range(bits - 1, low - 1, -1):
            bit = rest // 2 ** (b - low)
            there, rest = there + bit * turn[b], rest - bit * 2 ** (b - low)
        return there

    def at(base, r):
        x = UNROLL - 1 - r
        return sum((turn[b] for b in range(low) if x >> b & 1), base)

    def copy_k(owner, slot):
        return pltpu.make_async_copy(k_hbm.at[owner], kbuf.at[slot], ksem.at[slot])

    def copy_v(owner, slot):
        return pltpu.make_async_copy(v_hbm.at[owner], vbuf.at[slot], vsem.at[slot])

    def copy_piece(owner, slot, p):
        run = pl.ds(p * (tokens // PIECES), tokens // PIECES)
        return pltpu.make_async_copy(v_hbm.at[owner, :, run], vbuf.at[slot, :, run], psem.at[p])

    def remote(src, dst, ssem, rsem, there):
        return pltpu.make_async_remote_copy(src, dst, ssem, rsem, device_id={"sp": there}, device_id_type=MESH)

    def send_part(x, there, group):
        remote(seen_out.at[x], seen_in.at[x], part_ssem.at[0], seen_rsem.at[group], there).start()
        remote(stat_out.at[x], stat_in.at[x], part_ssem.at[1], stat_rsem.at[group], there).start()

    q_copy = pltpu.make_async_copy(q_hbm, q_ref, qsem)
    first = [peer(n - 1 - i) for i in range(SLOTS)]
    q_copy.start()
    copy_k(first[0], 0).start()
    for i in range(SLOTS - 1):
        copy_k(first[i + 1], i + 1).start()
        copy_v(first[i], i).start()
    copy_v(first[-1], SLOTS - 1).start()

    barrier = pltpu.get_barrier_semaphore()
    for x in range(1, n):
        pl.semaphore_signal(barrier, inc=1, device_id={"sp": peer(x)}, device_id_type=MESH)

    rows = lax.broadcasted_iota(jnp.int32, (2 * heads, LANES), 0)
    lanes = lax.broadcasted_iota(jnp.int32, (2 * heads, LANES), 1)
    bias = jnp.where(rows % heads == lanes % heads, 0.0, -jnp.inf).astype(jnp.float32)
    lane = lax.broadcasted_iota(jnp.int32, (heads // 2, LANES), 1)
    factor = scale * 1.4426950408889634

    def scores(owner, slot, s_ref):
        q = q_ref[owner]
        zero = jnp.zeros_like(q)
        q2 = jnp.concatenate([jnp.concatenate([q, zero], 1), jnp.concatenate([zero, q], 1)], 0)
        k = kbuf[slot].reshape(2, half, head)
        k2 = jnp.concatenate([k[0], k[1]], 1)
        s_ref[...] = lax.dot_general(q2, k2, (((1,), (1,)), ((), ())), preferred_element_type=jnp.float32)

    def weigh(s_ref):
        tiles = [s_ref[:, t : t + LANES] + bias for t in range(0, half, LANES)]
        high = functools.reduce(jnp.maximum, tiles)
        high = jnp.max(jnp.maximum(high[:heads], high[heads:]), 1, keepdims=True)
        both = jnp.concatenate([high, high], 0)
        weights = [jnp.exp2((t - both) * factor) for t in tiles]
        total = functools.reduce(jnp.add, weights)
        total = jnp.sum(total[:heads] + total[heads:], 1, keepdims=True)
        return jnp.concatenate([w.astype(jnp.bfloat16) for w in weights], 1), high, total

    def values(slot, weights, p=0, pieces=1):
        run = tokens // pieces
        v = vbuf[slot, :, p * run : (p + 1) * run].reshape(2, run * heads, head)
        v2 = jnp.concatenate([v[0], v[1]], 1)
        weights = weights[:, p * run * heads : (p + 1) * run * heads]
        seen = jnp.dot(weights, v2, preferred_element_type=jnp.float32)
        return seen[:heads, :head] + seen[heads:, head:]

    def part(slot, s_ref, x):
        weights, high, total = weigh(s_ref)
        seen = values(slot, weights)
        h = heads // 2
        seen_out[x] = seen.astype(jnp.bfloat16)
        stat_out[x] = jnp.where(lane < 32, high[:h], jnp.where(lane < 64, high[h:], jnp.where(lane < 96, total[:h], total[h:])))

    def wait_group(g):
        xs = pl.ds(groups[g].start, len(groups[g]))
        remote(stat_in.at[xs], stat_in.at[xs], part_ssem.at[1], stat_rsem.at[g], me).wait_recv()
        remote(seen_in.at[xs], seen_in.at[xs], part_ssem.at[0], seen_rsem.at[g], me).wait_recv()

    def spread(w, at):
        return jnp.concatenate([w[:, at : at + 1], w[:, at + 32 : at + 33]], 0)

    def absorb(g):
        stats = [stat_in[x] for x in groups[g]]
        top = functools.reduce(jnp.maximum, stats)
        sums = jnp.zeros((heads // 2, LANES), jnp.float32)
        acc = jnp.zeros((heads, head), jnp.float32)
        if g < len(groups) - 1:
            old = top_ref[...]
            top = jnp.maximum(top, old)
            w = jnp.exp2((old - top) * factor)
            sums = pltpu.roll(w, LANES // 2, 1) * sums_ref[...]
            acc = acc_ref[...] * spread(w, 0)
        for x, stat in zip(groups[g], stats):
            w = jnp.exp2((stat - top) * factor)
            sums += pltpu.roll(w, LANES // 2, 1) * stat
            acc += seen_in[x].astype(jnp.float32) * spread(w, 0)
        top_ref[...], sums_ref[...], acc_ref[...] = top, sums, acc

    def step(r, bases, s_now, s_next, slot, x, refill, pieces=False, group=None, send=None, sync=None):
        now, after, later = bases
        nxt = at(now, r + 1) if r + 1 < UNROLL else at(after, 0)
        k_slot = (slot + 1) % SLOTS if isinstance(slot, int) else (slot + 1 if (r + 1) % UNROLL else UNROLL - (slot - r))
        if refill:
            copy_k(at(later, r), slot).start()
            before = (slot - 1) % SLOTS if isinstance(slot, int) else (slot - 1 if r else 2 * UNROLL - 1 - slot)
            if r:
                copy_v(at(later, r - 1), before).start()
        with jax.named_scope("wait"):
            copy_k(nxt, k_slot).wait()
            copy_v(at(now, r), slot).wait()
            if group is not None:
                wait_group(group)
        with jax.named_scope("body"):
            scores(nxt, k_slot, s_next)
            part(slot, s_now, x)
            if group is not None:
                absorb(group)
        if refill and r == UNROLL - 1:
            copy_v(at(later, r), slot).start()
        if send is not None:
            send_part(x, at(now, r), send)

    with jax.named_scope("wait0"):
        q_copy.wait()
        copy_k(first[0], 0).wait()
    with jax.named_scope("score0"):
        scores(first[0], 0, s0)

    def steps(j, bases, refill, send, slot0):
        for r in range(UNROLL):
            x = n - 1 - (UNROLL * j + r)
            group = None
            if send:
                group = group_of(x) if isinstance(x, int) else send(j)
            step(r, bases, (s0, s1)[r % 2], (s0, s1)[(r + 1) % 2], slot0 + r, x, refill, send=group)

    for j in range(GREET // UNROLL):
        steps(j, (block(j), block(j + 1), block(j + SLOTS // UNROLL)), True, None, UNROLL * j % SLOTS)

    with jax.named_scope("barrier"):
        pl.semaphore_wait(barrier, n - 1)
    for i in range(GREET):
        x = n - 1 - i
        send_part(x, peer(x), group_of(x))

    for j in range(GREET // UNROLL, n // UNROLL):
        bases = (block(j), block(j + 1) if UNROLL * (j + 1) < n else None, block(j + SLOTS // UNROLL) if UNROLL * (j + SLOTS // UNROLL) < n else None)
        for r in range(UNROLL):
            i = UNROLL * j + r
            x = n - 1 - i
            if i == n - 1:
                break
            group = {n - 8: len(groups) - 1, n - 4: len(groups) - 2, n - 2: len(groups) - 3}.get(i)
            slot = i % SLOTS
            step(r, bases, (s0, s1)[r % 2], (s0, s1)[(r + 1) % 2], slot, x, bases[2] is not None, group=group, send=group_of(x))

    last = (n - 1) % SLOTS
    with jax.named_scope("ownweigh"):
        weights, high, total = weigh(s1)
    with jax.named_scope("waitparts"):
        wait_group(0)
    with jax.named_scope("combine"):
        absorb(0)
        top, sums = spread(top_ref[...], 0), spread(sums_ref[...], 64)
        new = jnp.maximum(top, high)
        theirs, ours = jnp.exp2((top - new) * factor), jnp.exp2((high - new) * factor)
        below = 1 / (sums * theirs + total * ours)
        acc, ours = acc_ref[...] * (theirs * below), ours * below
    with jax.named_scope("waitv"):
        copy_v(me, last).wait()
    with jax.named_scope("ownvalues"):
        mine[...] = (acc + values(last, weights) * ours).astype(jnp.bfloat16)

    with jax.named_scope("sendout"):
        for x in range(n - 1, 0, -1):
            remote(mine, out_ref.at[me], out_ssem, out_rsem, peer(x)).start()
        out_ref[me] = mine[...]

    with jax.named_scope("waitout"):
        every = pl.ds(1, n - 1)
        remote(seen_out.at[every], seen_out.at[every], part_ssem.at[0], out_rsem, me).wait_send()
        remote(stat_out.at[every], stat_out.at[every], part_ssem.at[1], out_rsem, me).wait_send()
        remote(out_ref.at[every], out_ref.at[every], out_ssem, out_rsem, me).wait()


def solution(mesh):
    n = mesh.shape["sp"]

    def step(q, k, v):
        batch, tokens, heads, head = k.shape
        shape = (batch, 2, tokens // 2, heads, head)
        rows = tokens * heads // 2
        return pl.pallas_call(
            functools.partial(kernel, n, head**-0.5),
            out_shape=pltpu.VMEM(q.shape, q.dtype),
            in_specs=[pl.BlockSpec(memory_space=pl.ANY)] * 3,
            out_specs=pl.BlockSpec(memory_space=pltpu.VMEM),
            scratch_shapes=[
                pltpu.VMEM(q.shape, q.dtype),
                pltpu.VMEM((SLOTS, *shape[1:]), k.dtype),
                pltpu.VMEM((SLOTS, *shape[1:]), v.dtype),
                pltpu.VMEM((2 * heads, rows), jnp.float32),
                pltpu.VMEM((2 * heads, rows), jnp.float32),
                pltpu.VMEM((n, heads, head), jnp.bfloat16),
                pltpu.VMEM((n, heads // 2, LANES), jnp.float32),
                pltpu.VMEM((n, heads, head), jnp.bfloat16),
                pltpu.VMEM((n, heads // 2, LANES), jnp.float32),
                pltpu.VMEM((heads, head), jnp.float32),
                pltpu.VMEM((heads // 2, LANES), jnp.float32),
                pltpu.VMEM((heads // 2, LANES), jnp.float32),
                pltpu.VMEM((heads, head), jnp.bfloat16),
                pltpu.SemaphoreType.DMA,
                pltpu.SemaphoreType.DMA((SLOTS,)),
                pltpu.SemaphoreType.DMA((SLOTS,)),
                pltpu.SemaphoreType.DMA((PIECES,)),
                pltpu.SemaphoreType.DMA((2,)),
                pltpu.SemaphoreType.DMA((4,)),
                pltpu.SemaphoreType.DMA((4,)),
                pltpu.SemaphoreType.DMA,
                pltpu.SemaphoreType.DMA,
            ],
            compiler_params=pltpu.CompilerParams(collective_id=0, has_side_effects=True, vmem_limit_bytes=60 * 2**20),
        )(q, k.reshape(shape), v.reshape(shape))

    return jax.shard_map(
        step,
        mesh=mesh,
        in_specs=(P("dp", None, None), P("dp", "sp", None, None), P("dp", "sp", None, None)),
        out_specs=P("dp", None, None),
        check_vma=False,
    )
```

time: 200 us -> 34.5 us (0.17)
  waiting for transfers between devices: 117 us -> 0 us
  matrix products: 37.3 us -> 0 us
  Pallas kernels: 0 us -> 33.7 us
  other arithmetic: 22.6 us -> 0 us
  between operations: 13.4 us -> 0.01 us
  local copies, waits for them, and re-layouts: 8.95 us -> 0.66 us
    all_gather x1 -> x0, waiting for transfers between devices: 117 us -> none  [step(): return together(lax.all_gather(part_of(q, k, v), 'sp')).reshape(q.shape)]
    dot_general x2 -> x0, matrix products: 37.3 us -> none  [einsum(): return jnp.einsum(form, a.astype(jnp.float32), b.astype(jnp.float32))]
    pallas_call x0 -> x1, Pallas kernels: none -> 33.7 us  [step(): pl.pallas_call(functools.partial(kernel, n, head ** (-0.5)), out_shape=pl...]
    reduce_sum x2 -> x0, other arithmetic: 14.8 us -> none  [the longest x1 9.47 us: together(): jnp.sum(total * scale, 0)]
    mul x1 -> x0, local copies, waits for them, and re-layouts: 8.43 us -> none  [together(): seen * scale]
    reduce_max x2 -> x0, other arithmetic: 5.84 us -> none  [the longest x1 5.69 us: together(): scale = jnp.exp(high - jnp.max(high, 0))]
  transfers between devices with their start and end apart: 1 -> 0, of which waited for: 1 -> 0; matrix products, arithmetic and copies ran while one was open for 0% -> 0% of each run, Pallas kernels for 0% -> 0%
where the time goes in v2:
time: 34.5 us; the launch traced here: 34.3 us
  Pallas kernels  33.7 us (98%)
  local copies, waits for them, and re-layouts  0.66 us (2%)
    pallas_call x1, Pallas kernels, step(): pl.pallas_call(functools.partial(kernel, n, head ** (-0.5)), out_shape=pl...  33.7 us

profile of v2, /device:TPU:0, one launch (start us, length us, event | category | flops | bytes accessed | tf_op | source)
XLA Modules:
  0.0 34.3 jit_solution(1812325582318513797)
XLA Ops:
  0.0 33.7 %shard_map.37 = bf16[32,16,128]{2,1,0:T(8,128)(2,1)S(1)} custom-call(bf16[32,16,128]{2,1,0:T(8,128)(2,1)} %q_hbm.1, bf16[32,2,128,16,128]{4,3,2,1,0:T(8,128)(2,1)} %bitcast.2, bf16[32,2,128,16,128]{4,3,2,1,0:T(8,128)(2,1)} %bitcast.3), custom_call_target="tpu_custom_call" | custom-call | tf_op jit(solution)/shard_map/pallas_call | solution.py:235
  33.7 0.7 %copy.5 = bf16[32,16,128]{2,1,0:T(8,128)(2,1)} copy(bf16[32,16,128]{2,1,0:T(8,128)(2,1)S(1)} %shard_map.37) | data formatting | bytes 262144

commit v3 on v0

v3 whole, which is shorter than its diff:
```python
import functools

import jax
import jax.numpy as jnp
from jax import lax
from jax.experimental import pallas as pl
from jax.experimental.pallas import tpu as pltpu
from jax.sharding import PartitionSpec as P

MESH = pl.DeviceIdType.MESH
K_SLOTS = 10
V_SLOTS = 10
GREET = 16
RUN = 2
BUFFERS = 4
FIRST = 2
PHASES = 2
LANES = 128


def distance(x):
    return bin(x >> 3).count("1") + (x >> 1 & 3)


def order_of(n):
    tail = [x for x in (2, 8, 3, 9, 16, 17, 1, 0) if x < n]
    return sorted((x for x in range(n) if x not in tail), key=lambda x: (-distance(x), -x)) + tail


def kernel(n, scale, q_hbm, k_hbm, v_hbm, out_ref, q_ref, kbuf, vbuf, s_refs, p_refs, seen_out, stat_out, seen_in, stat_in, acc_ref, top_ref, sums_ref, own_ref, mine, qsem, ksem, vsem, part_ssem, seen_rsem, stat_rsem, out_ssem, out_rsem):
    me = lax.axis_index("sp")
    batch, tokens, phases, heads, head = k_hbm.shape
    half = tokens * heads // 2
    units = n * phases
    bits = (n - 1).bit_length()
    order = order_of(n)
    turn = [(1 - 2 * ((me // 2**b) % 2)) * 2**b for b in range(bits)]
    sizes = [1, 1] + [RUN] * ((units - 6) // RUN) + [1] * 4
    assert sum(sizes) == units
    starts = [sum(sizes[:b]) for b in range(len(sizes) + 1)]
    blocks = [list(range(a, b)) for a, b in zip(starts, starts[1:])] + [[], []]
    cuts = [0, n // 2, n - n // 4, n]

    def peer(x):
        return sum((turn[b] for b in range(bits) if x >> b & 1), me)

    def owner(u):
        return peer(order[u % n])

    def group_of(i):
        return sum(i >= cut for cut in cuts[1:-1])

    def copy_k(u):
        slot = u % K_SLOTS
        return pltpu.make_async_copy(k_hbm.at[owner(u), :, u // n], kbuf.at[slot], ksem.at[slot])

    def copy_v(u):
        slot = u % V_SLOTS
        return pltpu.make_async_copy(v_hbm.at[owner(u), :, u // n], vbuf.at[slot], vsem.at[slot])

    def remote(src, dst, ssem, rsem, there):
        return pltpu.make_async_remote_copy(src, dst, ssem, rsem, device_id={"sp": there}, device_id_type=MESH)

    def send_part(u):
        f, i = divmod(u, n)
        g, row = group_of(i), pl.ds(i, 1)
        remote(stat_out.at[f, row], stat_in.at[f, row], part_ssem.at[1], stat_rsem.at[f, g], owner(u)).start()
        remote(seen_out.at[f, i], seen_in.at[f, i], part_ssem.at[0], seen_rsem.at[f, g], owner(u)).start()

    q_copy = pltpu.make_async_copy(q_hbm, q_ref, qsem)
    q_copy.start()
    stream = [(copy_k, u) for u in blocks[0] + blocks[1]]
    for b in range(len(sizes)):
        stream += [(copy_k, u) for u in blocks[b + 2]] + [(copy_v, u) for u in blocks[b]]
    stream = [(copy, u) for copy, u in stream if u < (K_SLOTS if copy is copy_k else V_SLOTS)]
    for copy, u in stream[:3]:
        copy(u).start()

    barrier = pltpu.get_barrier_semaphore()
    for x in range(1, n):
        pl.semaphore_signal(barrier, inc=1, device_id={"sp": peer(x)}, device_id_type=MESH)

    for copy, u in stream[3:]:
        copy(u).start()

    rows = lax.broadcasted_iota(jnp.int32, (2 * heads, LANES), 0)
    lanes = lax.broadcasted_iota(jnp.int32, (2 * heads, LANES), 1)
    bias = jnp.where(rows % heads == lanes % heads, 0.0, -jnp.inf).astype(jnp.float32)
    sub = lax.broadcasted_iota(jnp.int32, (heads, LANES), 0)
    lane = lax.broadcasted_iota(jnp.int32, (heads, LANES), 1)
    factor = scale * 1.4426950408889634

    def scores(u):
        f = u // n
        q = q_ref[owner(u)].astype(jnp.float32)[f * heads : (f + 1) * heads]
        zero = jnp.zeros_like(q)
        q2 = jnp.concatenate([jnp.concatenate([q, zero], 1), jnp.concatenate([zero, q], 1)], 0).astype(jnp.bfloat16)
        k = kbuf[u % K_SLOTS].reshape(2, half, head)
        k2 = jnp.concatenate([k[0], k[1]], 1)
        s_refs[u % BUFFERS][...] = lax.dot_general(q2, k2, (((1,), (1,)), ((), ())), preferred_element_type=jnp.float32)

    def weigh(u):
        f, i = divmod(u, n)
        s_ref, p_ref = s_refs[u % BUFFERS], p_refs[u % BUFFERS]
        tiles = [s_ref[:, t : t + LANES] + bias for t in range(0, half, LANES)]
        high = functools.reduce(jnp.maximum, tiles)
        high = jnp.max(jnp.maximum(high[:heads], high[heads:]), 1, keepdims=True)
        both = jnp.concatenate([high, high], 0)
        weights = [jnp.exp2((t - both) * factor) for t in tiles]
        total = functools.reduce(jnp.add, weights)
        total = jnp.sum(total[:heads] + total[heads:], 1, keepdims=True)
        for t, w in enumerate(weights):
            p_ref[:, t * LANES : (t + 1) * LANES] = w.astype(jnp.bfloat16)
        stat = jnp.sum(jnp.where(lane == sub, high, jnp.where(lane == sub + heads, total, 0.0)), 0, keepdims=True)
        if i == n - 1:
            stat_in[f, i : i + 1] = stat
        else:
            stat_out[f, i : i + 1] = stat

    def values(u):
        v = vbuf[u % V_SLOTS].reshape(2, half, head)
        v2 = jnp.concatenate([v[0], v[1]], 1)
        seen = jnp.dot(p_refs[u % BUFFERS][...], v2, preferred_element_type=jnp.float32)
        return seen[:heads, :head] + seen[heads:, head:]

    def wait_group(f, g):
        run = pl.ds(cuts[g], min(cuts[g + 1], n - 1) - cuts[g])
        remote(stat_in.at[f, run], stat_in.at[f, run], part_ssem.at[1], stat_rsem.at[f, g], me).wait_recv()
        remote(seen_in.at[f, run], seen_in.at[f, run], part_ssem.at[0], seen_rsem.at[f, g], me).wait_recv()

    def column(row, first=0):
        return jnp.sum(jnp.where(lane == sub + first, row, 0.0), 1, keepdims=True)

    def absorb(f, g):
        stats = stat_in[f, cuts[g] : cuts[g + 1]]
        top = jnp.max(stats, 0, keepdims=True)
        if g:
            old = top_ref[f]
            top = jnp.maximum(top, old)
        w = jnp.exp2((stats - top) * factor)
        sums = jnp.sum(pltpu.roll(w, heads, 1) * stats, 0, keepdims=True)
        acc = jnp.zeros((heads, head), jnp.float32)
        if g:
            scaled = jnp.exp2((old - top) * factor)
            sums += pltpu.roll(scaled, heads, 1) * sums_ref[f]
            acc = acc_ref[f] * column(scaled)
        for i in range(cuts[g], min(cuts[g + 1], n - 1)):
            row = i - cuts[g]
            acc += seen_in[f, i].astype(jnp.float32) * column(w[row : row + 1])
        if cuts[g + 1] < n:
            top_ref[f], sums_ref[f], acc_ref[f] = top, sums, acc
            return None
        below = 1 / column(sums, heads)
        return acc * below, column(w[n - 1 - cuts[g] : n - cuts[g]]) * below

    def finish(f):
        run = pl.ds(f * heads, heads)

        def send(there):
            remote(mine.at[f], out_ref.at[me, run], out_ssem, out_rsem.at[f], there).start()

        for there in range(FIRST):
            pl.when(me != there)(functools.partial(send, there))
        for x in order[:-1]:
            there = peer(x)
            pl.when(there >= FIRST)(functools.partial(send, there))
        out_ref[me, run] = mine[f]

    def refill(ks, vs):
        for u in ks:
            if u + K_SLOTS < units:
                copy_k(u + K_SLOTS).start()
        for u in vs:
            if u + V_SLOTS < units:
                copy_v(u + V_SLOTS).start()

    with jax.named_scope("wait0"):
        q_copy.wait()
        for u in blocks[0]:
            copy_k(u).wait()
    with jax.named_scope("score0"):
        for u in blocks[0]:
            scores(u)
    refill(blocks[0], [])
    with jax.named_scope("wait1"):
        for u in blocks[1]:
            copy_k(u).wait()
    with jax.named_scope("score1"):
        for u in blocks[1]:
            scores(u)
        for u in blocks[0]:
            weigh(u)

    spare = {n + 12: (0, 0), n + 13: (0, 1), n + 15: (0, 2), units - 2: (1, 0)}
    sent = 0
    for b in range(len(sizes)):
        now, soon, later = blocks[b : b + 3]
        if now[0] >= GREET and not sent:
            with jax.named_scope("barrier"):
                pl.semaphore_wait(barrier, n - 1)
            for u in range(now[0]):
                send_part(u)
            sent = now[0]
        refill(soon, blocks[b - 1] if b else [])
        groups = [spare[u] for u in now if u in spare]
        with jax.named_scope("wait"):
            for u in later:
                copy_k(u).wait()
            for u in now:
                copy_v(u).wait()
            for group in groups:
                wait_group(*group)
        with jax.named_scope("body"):
            for u in now:
                f, i = divmod(u, n)
                seen = values(u)
                if i < n - 1:
                    seen_out[f, i] = seen.astype(jnp.bfloat16)
                else:
                    own_ref[...] = seen
            for u in soon:
                weigh(u)
            for u in later:
                scores(u)
            for group in groups:
                done = absorb(*group)
                if done is not None:
                    mine[group[0]] = (done[0] + own_ref[...] * done[1]).astype(jnp.bfloat16)
        if sent:
            for u in now:
                if u % n < n - 1:
                    send_part(u)
        for group in groups:
            if group[1] == 2:
                finish(group[0])

    with jax.named_scope("waitparts1"):
        wait_group(phases - 1, 1)
    with jax.named_scope("combine1"):
        absorb(phases - 1, 1)
    with jax.named_scope("waitparts"):
        wait_group(phases - 1, 2)
    with jax.named_scope("combine"):
        rest, share = absorb(phases - 1, 2)
        mine[phases - 1] = (rest + own_ref[...] * share).astype(jnp.bfloat16)
    with jax.named_scope("sendout"):
        finish(phases - 1)

    with jax.named_scope("waitout"):
        every = pl.ds(0, n - 1)
        for f in range(phases):
            remote(seen_out.at[f, every], seen_out.at[f, every], part_ssem.at[0], out_rsem.at[f], me).wait_send()
            remote(stat_out.at[f, every], stat_out.at[f, every], part_ssem.at[1], out_rsem.at[f], me).wait_send()
        for f in range(phases):
            landed = out_ref.at[every, pl.ds(f * heads, heads)]
            remote(landed, landed, out_ssem, out_rsem.at[f], me).wait()


def solution(mesh):
    n = mesh.shape["sp"]

    def step(q, k, v):
        batch, tokens, heads, head = k.shape
        heads //= PHASES
        half = tokens * heads // 2
        shape = (batch, tokens, PHASES, heads, head)
        return pl.pallas_call(
            functools.partial(kernel, n, head**-0.5),
            out_shape=pltpu.VMEM(q.shape, q.dtype),
            in_specs=[pl.BlockSpec(memory_space=pl.ANY)] * 3,
            out_specs=pl.BlockSpec(memory_space=pltpu.VMEM),
            scratch_shapes=[
                pltpu.VMEM(q.shape, q.dtype),
                pltpu.VMEM((K_SLOTS, tokens, heads, head), k.dtype),
                pltpu.VMEM((V_SLOTS, tokens, heads, head), v.dtype),
                [pltpu.VMEM((2 * heads, half), jnp.float32)] * BUFFERS,
                [pltpu.VMEM((2 * heads, half), jnp.bfloat16)] * BUFFERS,
                pltpu.VMEM((PHASES, n, heads, head), jnp.bfloat16),
                pltpu.VMEM((PHASES, n, LANES), jnp.float32),
                pltpu.VMEM((PHASES, n, heads, head), jnp.bfloat16),
                pltpu.VMEM((PHASES, n, LANES), jnp.float32),
                pltpu.VMEM((PHASES, heads, head), jnp.float32),
                pltpu.VMEM((PHASES, 1, LANES), jnp.float32),
                pltpu.VMEM((PHASES, 1, LANES), jnp.float32),
                pltpu.VMEM((heads, head), jnp.float32),
                pltpu.VMEM((PHASES, heads, head), jnp.bfloat16),
                pltpu.SemaphoreType.DMA,
                pltpu.SemaphoreType.DMA((K_SLOTS,)),
                pltpu.SemaphoreType.DMA((V_SLOTS,)),
                pltpu.SemaphoreType.DMA((2,)),
                pltpu.SemaphoreType.DMA((PHASES, 3)),
                pltpu.SemaphoreType.DMA((PHASES, 3)),
                pltpu.SemaphoreType.DMA,
                pltpu.SemaphoreType.DMA((PHASES,)),
            ],
            compiler_params=pltpu.CompilerParams(collective_id=0, has_side_effects=True, vmem_limit_bytes=60 * 2**20),
        )(q, k.reshape(shape), v.reshape(shape))

    return jax.shard_map(
        step,
        mesh=mesh,
        in_specs=(P("dp", None, None), P("dp", "sp", None, None), P("dp", "sp", None, None)),
        out_specs=P("dp", None, None),
        check_vma=False,
    )
```

time: 200 us -> 32.5 us (0.16)
  waiting for transfers between devices: 117 us -> 0 us
  matrix products: 37.3 us -> 0 us
  Pallas kernels: 0 us -> 31.7 us
  other arithmetic: 22.6 us -> 0 us
  between operations: 13.4 us -> 0.01 us
  local copies, waits for them, and re-layouts: 8.95 us -> 0.66 us
    all_gather x1 -> x0, waiting for transfers between devices: 117 us -> none  [step(): return together(lax.all_gather(part_of(q, k, v), 'sp')).reshape(q.shape)]
    dot_general x2 -> x0, matrix products: 37.3 us -> none  [einsum(): return jnp.einsum(form, a.astype(jnp.float32), b.astype(jnp.float32))]
    pallas_call x0 -> x1, Pallas kernels: none -> 31.7 us  [step(): pl.pallas_call(functools.partial(kernel, n, head ** (-0.5)), out_shape=pl...]
    reduce_sum x2 -> x0, other arithmetic: 14.8 us -> none  [the longest x1 9.47 us: together(): jnp.sum(total * scale, 0)]
    mul x1 -> x0, local copies, waits for them, and re-layouts: 8.43 us -> none  [together(): seen * scale]
    reduce_max x2 -> x0, other arithmetic: 5.84 us -> none  [the longest x1 5.69 us: together(): scale = jnp.exp(high - jnp.max(high, 0))]
  transfers between devices with their start and end apart: 1 -> 0, of which waited for: 1 -> 0; matrix products, arithmetic and copies ran while one was open for 0% -> 0% of each run, Pallas kernels for 0% -> 0%
where the time goes in v3:
time: 32.5 us; the launch traced here: 32.4 us
  Pallas kernels  31.7 us (98%)
  local copies, waits for them, and re-layouts  0.66 us (2%)
    pallas_call x1, Pallas kernels, step(): pl.pallas_call(functools.partial(kernel, n, head ** (-0.5)), out_shape=pl...  31.7 us
    unnamed x1, local copies, waits for them, and re-layouts  0.66 us

profile of v3, /device:TPU:0, one launch (start us, length us, event | category | flops | bytes accessed | tf_op | source)
XLA Modules:
  0.0 32.4 jit_solution(10642533843718159390)
XLA Ops:
  0.0 31.7 %shard_map.37 = bf16[32,16,128]{2,1,0:T(8,128)(2,1)S(1)} custom-call(bf16[32,16,128]{2,1,0:T(8,128)(2,1)} %q_hbm.1, bf16[32,256,2,8,128]{4,3,2,1,0:T(8,128)(2,1)} %bitcast.2, bf16[32,256,2,8,128]{4,3,2,1,0:T(8,128)(2,1)} %bitcast.3), custom_call_target="tpu_custom_call" | custom-call | tf_op jit(solution)/shard_map/pallas_call | solution.py:267
  31.7 0.7 %copy.5 = bf16[32,16,128]{2,1,0:T(8,128)(2,1)} copy(bf16[32,16,128]{2,1,0:T(8,128)(2,1)S(1)} %shard_map.37) | data formatting | bytes 262144

commit v4 on v3

v4 whole, which is shorter than its diff:
```python
import functools

import jax
import jax.numpy as jnp
from jax import lax
from jax.experimental import pallas as pl
from jax.experimental.pallas import tpu as pltpu
from jax.sharding import PartitionSpec as P

MESH = pl.DeviceIdType.MESH
K_SLOTS = 10
V_SLOTS = 10
GREET = 16
RUN = 2
BUFFERS = 4
FIRST = 2
PHASES = 2
LANES = 128


def distance(x):
    return bin(x >> 3).count("1") + (x >> 1 & 3)


def order_of(n):
    tail = [x for x in (2, 8, 3, 9, 16, 17, 1, 0) if x < n]
    return sorted((x for x in range(n) if x not in tail), key=lambda x: (-distance(x), -x)) + tail


def kernel(n, scale, q_hbm, k_hbm, v_hbm, out_ref, q_ref, kbuf, vbuf, s_refs, p_refs, part_out, part_in, acc_ref, top_ref, sums_ref, own_ref, qsem, ksem, vsem, part_ssem, part_rsem, out_ssem, out_rsem):
    me = lax.axis_index("sp")
    batch, tokens, phases, heads, head = k_hbm.shape
    half = tokens * heads // 2
    units = n * phases
    both_heads = phases * heads
    bits = (n - 1).bit_length()
    order = order_of(n)
    turn = [(1 - 2 * ((me // 2**b) % 2)) * 2**b for b in range(bits)]
    sizes = [1, 1] + [RUN] * ((units - 6) // RUN) + [1] * 4
    assert sum(sizes) == units
    starts = [sum(sizes[:b]) for b in range(len(sizes) + 1)]
    blocks = [list(range(a, b)) for a, b in zip(starts, starts[1:])] + [[], []]
    cuts = [0, n // 2, n - n // 4, n]

    def peer(x):
        return sum((turn[b] for b in range(bits) if x >> b & 1), me)

    def owner(u):
        return peer(order[u // phases])

    def group_of(i):
        return sum(i >= cut for cut in cuts[1:-1])

    def copy_k(u):
        slot = u % K_SLOTS
        return pltpu.make_async_copy(k_hbm.at[owner(u), :, u % phases], kbuf.at[slot], ksem.at[slot])

    def copy_v(u):
        slot = u % V_SLOTS
        return pltpu.make_async_copy(v_hbm.at[owner(u), :, u % phases], vbuf.at[slot], vsem.at[slot])

    def remote(src, dst, ssem, rsem, there):
        return pltpu.make_async_remote_copy(src, dst, ssem, rsem, device_id={"sp": there}, device_id_type=MESH)

    def send_part(i):
        remote(part_out.at[i], part_in.at[i], part_ssem, part_rsem.at[group_of(i)], peer(order[i])).start()

    q_copy = pltpu.make_async_copy(q_hbm, q_ref, qsem)
    q_copy.start()
    stream = [(copy_k, u) for u in blocks[0] + blocks[1]]
    for b in range(len(sizes)):
        stream += [(copy_k, u) for u in blocks[b + 2]] + [(copy_v, u) for u in blocks[b]]
    stream = [(copy, u) for copy, u in stream if u < (K_SLOTS if copy is copy_k else V_SLOTS)]
    for copy, u in stream[:3]:
        copy(u).start()

    barrier = pltpu.get_barrier_semaphore()
    for x in range(1, n):
        pl.semaphore_signal(barrier, inc=1, device_id={"sp": peer(x)}, device_id_type=MESH)

    for copy, u in stream[3:]:
        copy(u).start()

    rows = lax.broadcasted_iota(jnp.int32, (2 * heads, LANES), 0)
    lanes = lax.broadcasted_iota(jnp.int32, (2 * heads, LANES), 1)
    bias = jnp.where(rows % heads == lanes % heads, 0.0, -jnp.inf).astype(jnp.float32)
    sub = lax.broadcasted_iota(jnp.int32, (heads, LANES), 0)
    lane = lax.broadcasted_iota(jnp.int32, (heads, LANES), 1)
    factor = scale * 1.4426950408889634

    def scores(u):
        f = u % phases
        q = q_ref[owner(u)].astype(jnp.float32)[f * heads : (f + 1) * heads]
        zero = jnp.zeros_like(q)
        q2 = jnp.concatenate([jnp.concatenate([q, zero], 1), jnp.concatenate([zero, q], 1)], 0).astype(jnp.bfloat16)
        k = kbuf[u % K_SLOTS].reshape(2, half, head)
        k2 = jnp.concatenate([k[0], k[1]], 1)
        s_refs[u % BUFFERS][...] = lax.dot_general(q2, k2, (((1,), (1,)), ((), ())), preferred_element_type=jnp.float32)

    def weigh(u):
        i, f = divmod(u, phases)
        s_ref, p_ref = s_refs[u % BUFFERS], p_refs[u % BUFFERS]
        tiles = [s_ref[:, t : t + LANES] + bias for t in range(0, half, LANES)]
        high = functools.reduce(jnp.maximum, tiles)
        high = jnp.max(jnp.maximum(high[:heads], high[heads:]), 1, keepdims=True)
        both = jnp.concatenate([high, high], 0)
        weights = [jnp.exp2((t - both) * factor) for t in tiles]
        total = functools.reduce(jnp.add, weights)
        total = jnp.sum(total[:heads] + total[heads:], 1, keepdims=True)
        for t, w in enumerate(weights):
            p_ref[:, t * LANES : (t + 1) * LANES] = w.astype(jnp.bfloat16)
        stat = jnp.sum(jnp.where(lane == sub, high, jnp.where(lane == sub + heads, total, 0.0)), 0, keepdims=True)
        (part_in if i == n - 1 else part_out)[i, both_heads + f : both_heads + f + 1] = stat

    def values(u):
        v = vbuf[u % V_SLOTS].reshape(2, half, head)
        v2 = jnp.concatenate([v[0], v[1]], 1)
        seen = jnp.dot(p_refs[u % BUFFERS][...], v2, preferred_element_type=jnp.float32)
        return seen[:heads, :head] + seen[heads:, head:]

    def wait_group(g):
        run = pl.ds(cuts[g], min(cuts[g + 1], n - 1) - cuts[g])
        remote(part_in.at[run], part_in.at[run], part_ssem, part_rsem.at[g], me).wait_recv()

    def column(stat, first=0):
        picked = [jnp.where(lane == sub + first, stat[f : f + 1], 0.0) for f in range(phases)]
        return jnp.sum(jnp.concatenate(picked, 0), 1, keepdims=True)

    def absorb(g):
        stats = [part_in[i, both_heads:] for i in range(cuts[g], cuts[g + 1])]
        top = functools.reduce(jnp.maximum, stats)
        sums = jnp.zeros_like(top)
        acc = jnp.zeros((both_heads, head), jnp.float32)
        if g:
            old = top_ref[...]
            top = jnp.maximum(top, old)
            scaled = jnp.exp2((old - top) * factor)
            sums = pltpu.roll(scaled, heads, 1) * sums_ref[...]
            acc = acc_ref[...] * column(scaled)
        for i, stat in zip(range(cuts[g], cuts[g + 1]), stats):
            w = jnp.exp2((stat - top) * factor)
            sums += pltpu.roll(w, heads, 1) * stat
            acc += (own_ref[...] if i == n - 1 else part_in[i, :both_heads]) * column(w)
        if cuts[g + 1] == n:
            return (acc / column(sums, heads)).astype(jnp.bfloat16)
        top_ref[...], sums_ref[...], acc_ref[...] = top, sums, acc

    def refill(ks, vs):
        for u in ks:
            if u + K_SLOTS < units:
                copy_k(u + K_SLOTS).start()
        for u in vs:
            if u + V_SLOTS < units:
                copy_v(u + V_SLOTS).start()

    with jax.named_scope("wait0"):
        q_copy.wait()
        for u in blocks[0]:
            copy_k(u).wait()
    with jax.named_scope("score0"):
        for u in blocks[0]:
            scores(u)
    refill(blocks[0], [])
    with jax.named_scope("wait1"):
        for u in blocks[1]:
            copy_k(u).wait()
    with jax.named_scope("score1"):
        for u in blocks[1]:
            scores(u)
        for u in blocks[0]:
            weigh(u)

    spare = {units - 2: 0}
    sent = 0
    for b in range(len(sizes)):
        now, soon, later = blocks[b : b + 3]
        if now[0] >= GREET and not sent:
            with jax.named_scope("barrier"):
                pl.semaphore_wait(barrier, n - 1)
            for i in range(now[0] // phases):
                send_part(i)
            sent = now[0]
        refill(soon, blocks[b - 1] if b else [])
        groups = [spare[u] for u in now if u in spare]
        with jax.named_scope("wait"):
            for u in later:
                copy_k(u).wait()
            for u in now:
                copy_v(u).wait()
            for group in groups:
                wait_group(group)
        with jax.named_scope("body"):
            for u in now:
                i, f = divmod(u, phases)
                run = pl.ds(f * heads, heads)
                if i < n - 1:
                    part_out[i, run] = values(u)
                else:
                    own_ref[run] = values(u)
            for u in soon:
                weigh(u)
            for u in later:
                scores(u)
            for group in groups:
                absorb(group)
        if sent:
            for u in now:
                if u % phases == phases - 1 and u < units - phases:
                    send_part(u // phases)

    with jax.named_scope("waitparts1"):
        wait_group(1)
    with jax.named_scope("combine1"):
        absorb(1)
    with jax.named_scope("waitparts"):
        wait_group(2)
    with jax.named_scope("combine"):
        out_ref[me] = absorb(2)

    with jax.named_scope("sendout"):

        def send(there):
            remote(out_ref.at[me], out_ref.at[me], out_ssem, out_rsem, there).start()

        for there in range(FIRST):
            pl.when(me != there)(functools.partial(send, there))
        for x in order[:-1]:
            there = peer(x)
            pl.when(there >= FIRST)(functools.partial(send, there))
    with jax.named_scope("waitout"):
        landed = out_ref.at[pl.ds(0, n - 1)]
        remote(landed, landed, out_ssem, out_rsem, me).wait()
    with jax.named_scope("waitsends"):
        every = pl.ds(0, n - 1)
        remote(part_out.at[every], part_out.at[every], part_ssem, part_rsem.at[0], me).wait_send()


def solution(mesh):
    n = mesh.shape["sp"]

    def step(q, k, v):
        batch, tokens, heads, head = k.shape
        heads //= PHASES
        half = tokens * heads // 2
        shape = (batch, tokens, PHASES, heads, head)
        return pl.pallas_call(
            functools.partial(kernel, n, head**-0.5),
            out_shape=pltpu.VMEM(q.shape, q.dtype),
            in_specs=[pl.BlockSpec(memory_space=pl.ANY)] * 3,
            out_specs=pl.BlockSpec(memory_space=pltpu.VMEM),
            scratch_shapes=[
                pltpu.VMEM(q.shape, q.dtype),
                pltpu.VMEM((K_SLOTS, tokens, heads, head), k.dtype),
                pltpu.VMEM((V_SLOTS, tokens, heads, head), v.dtype),
                [pltpu.VMEM((2 * heads, half), jnp.float32)] * BUFFERS,
                [pltpu.VMEM((2 * heads, half), jnp.bfloat16)] * BUFFERS,
                pltpu.VMEM((n, PHASES * heads + PHASES, LANES), jnp.float32),
                pltpu.VMEM((n, PHASES * heads + PHASES, LANES), jnp.float32),
                pltpu.VMEM((PHASES * heads, head), jnp.float32),
                pltpu.VMEM((PHASES, LANES), jnp.float32),
                pltpu.VMEM((PHASES, LANES), jnp.float32),
                pltpu.VMEM((PHASES * heads, head), jnp.float32),
                pltpu.SemaphoreType.DMA,
                pltpu.SemaphoreType.DMA((K_SLOTS,)),
                pltpu.SemaphoreType.DMA((V_SLOTS,)),
                pltpu.SemaphoreType.DMA,
                pltpu.SemaphoreType.DMA((3,)),
                pltpu.SemaphoreType.DMA,
                pltpu.SemaphoreType.DMA,
            ],
            compiler_params=pltpu.CompilerParams(collective_id=0, has_side_effects=True, vmem_limit_bytes=60 * 2**20),
        )(q, k.reshape(shape), v.reshape(shape))

    return jax.shard_map(
        step,
        mesh=mesh,
        in_specs=(P("dp", None, None), P("dp", "sp", None, None), P("dp", "sp", None, None)),
        out_specs=P("dp", None, None),
        check_vma=False,
    )
```

time: 32.5 us -> 31.5 us (0.969)
  Pallas kernels: 31.7 us -> 30.7 us
    pallas_call x1, Pallas kernels: 31.7 us -> 30.7 us  [step(): pl.pallas_call(functools.partial(kernel, n, head ** (-0.5)), out_shape=pl...]
where the time goes in v4:
time: 31.5 us; the launch traced here: 31.3 us
  Pallas kernels  30.7 us (97%)
  local copies, waits for them, and re-layouts  0.66 us (2%)
    pallas_call x1, Pallas kernels, step(): pl.pallas_call(functools.partial(kernel, n, head ** (-0.5)), out_shape=pl...  30.7 us
    unnamed x1, local copies, waits for them, and re-layouts  0.66 us

profile of v4, /device:TPU:0, one launch (start us, length us, event | category | flops | bytes accessed | tf_op | source)
XLA Modules:
  0.0 31.3 jit_solution(4953631555208373768)
XLA Ops:
  0.0 30.7 %shard_map.37 = bf16[32,16,128]{2,1,0:T(8,128)(2,1)S(1)} custom-call(bf16[32,16,128]{2,1,0:T(8,128)(2,1)} %q_hbm.1, bf16[32,256,2,8,128]{4,3,2,1,0:T(8,128)(2,1)} %bitcast.2, bf16[32,256,2,8,128]{4,3,2,1,0:T(8,128)(2,1)} %bitcast.3), custom_call_target="tpu_custom_call" | custom-call | tf_op jit(solution)/shard_map/pallas_call | solution.py:246
  30.7 0.7 %copy.5 = bf16[32,16,128]{2,1,0:T(8,128)(2,1)} copy(bf16[32,16,128]{2,1,0:T(8,128)(2,1)S(1)} %shard_map.37) | data formatting | bytes 262144

commit v5 on v4

--- a/solution.py
+++ b/solution.py
@@ -40,7 +40,7 @@
     assert sum(sizes) == units
     starts = [sum(sizes[:b]) for b in range(len(sizes) + 1)]
     blocks = [list(range(a, b)) for a, b in zip(starts, starts[1:])] + [[], []]
-    cuts = [0, n // 2, n - n // 4, n]
+    cuts = [0, n // 2, n - n // 4, n - n // 8, n]
 
     def peer(x):
         return sum((turn[b] for b in range(bits) if x >> b & 1), me)
@@ -170,7 +170,7 @@
         for u in blocks[0]:
             weigh(u)
 
-    spare = {units - 2: 0}
+    spare = {units - 2: 0, units - 1: 1}
     sent = 0
     for b in range(len(sizes)):
         now, soon, later = blocks[b : b + 3]
@@ -209,13 +209,13 @@
                     send_part(u // phases)
 
     with jax.named_scope("waitparts1"):
-        wait_group(1)
+        wait_group(2)
     with jax.named_scope("combine1"):
-        absorb(1)
+        absorb(2)
     with jax.named_scope("waitparts"):
-        wait_group(2)
+        wait_group(3)
     with jax.named_scope("combine"):
-        out_ref[me] = absorb(2)
+        out_ref[me] = absorb(3)
 
     with jax.named_scope("sendout"):
 
@@ -264,7 +264,7 @@
                 pltpu.SemaphoreType.DMA((K_SLOTS,)),
                 pltpu.SemaphoreType.DMA((V_SLOTS,)),
                 pltpu.SemaphoreType.DMA,
-                pltpu.SemaphoreType.DMA((3,)),
+                pltpu.SemaphoreType.DMA((4,)),
                 pltpu.SemaphoreType.DMA,
                 pltpu.SemaphoreType.DMA,
             ],

time: 31.5 us -> 31.5 us (level)
  no operation moved by 1% of the time
where the time goes in v5:
time: 31.5 us; the launch traced here: 31.3 us
  Pallas kernels  30.7 us (97%)
  local copies, waits for them, and re-layouts  0.66 us (2%)
    pallas_call x1, Pallas kernels, step(): pl.pallas_call(functools.partial(kernel, n, head ** (-0.5)), out_shape=pl...  30.7 us
    unnamed x1, local copies, waits for them, and re-layouts  0.66 us

profile of v5, /device:TPU:0, one launch (start us, length us, event | category | flops | bytes accessed | tf_op | source)
XLA Modules:
  0.0 31.3 jit_solution(2244778021640317016)
XLA Ops:
  0.0 30.7 %shard_map.37 = bf16[32,16,128]{2,1,0:T(8,128)(2,1)S(1)} custom-call(bf16[32,16,128]{2,1,0:T(8,128)(2,1)} %q_hbm.1, bf16[32,256,2,8,128]{4,3,2,1,0:T(8,128)(2,1)} %bitcast.2, bf16[32,256,2,8,128]{4,3,2,1,0:T(8,128)(2,1)} %bitcast.3), custom_call_target="tpu_custom_call" | custom-call | tf_op jit(solution)/shard_map/pallas_call | solution.py:246
  30.7 0.7 %copy.5 = bf16[32,16,128]{2,1,0:T(8,128)(2,1)} copy(bf16[32,16,128]{2,1,0:T(8,128)(2,1)S(1)} %shard_map.37) | data formatting | bytes 262144
